TPU v7x, 32 devices: a whole 2x2x4 slice. The times are simulated.
32 devices in a mesh: pix: 8 (over y, x, core), row: 4 (over z).
Axes of the slice: x: 2, y: 2, z: 4, core: 2. Of those that a mesh axis runs over, the one named last changes fastest.
Arguments:
- band_images: bfloat16 [256, 128, 512], P('pix', 'row'), may hold values from -6 to 6
- pivots: int32 [2, 32], replicated, may hold values from 0 to 65535, as said below
Outputs:
- residual: bfloat16 [512, 128, 256], P(('pix', 'row'))
- coefficients: bfloat16 [64, 512, 128], P(None, ('pix', 'row'))
Inputs may be any that keep to these rules, and one draw needn't show every extreme that they name: All 64 pivots lie in different columns, and every group of 32 lines starting at a multiple of 32 holds at least one pivot.
All inputs are finite; a program needn't handle non-finite values.
Results may differ from a plain program's by a relative error of at most 0.001.
Values may be sent and summed in bfloat16 or wider, within the bound.
No kernel may reach another device: no remote copies, remote signals or barrier semaphores. Data moves between devices by JAX's collectives and lax.ppermute only.
A program may use at most 192 MiB of HBM per device.

v0:
```python
import jax
import jax.numpy as jnp
from jax import lax
from jax.experimental import pallas as pl
from jax.experimental.pallas import tpu as pltpu
from jax.sharding import PartitionSpec as P


highest = lax.Precision.HIGHEST
f32 = jnp.float32
bf16 = jnp.bfloat16
LANES = 128
SUBLANES = 8
AXES = ("pix", "row")


def contract_last(a, b):
    return lax.dot_general(a, b, (((1,), (1,)), ((), ())), preferred_element_type=f32)


def hot(shape, test):
    row = lax.broadcasted_iota(jnp.int32, shape, 0)
    column = lax.broadcasted_iota(jnp.int32, shape, 1)
    return test(row, column).astype(f32).astype(bf16)


def swap_rows(outer, inner):
    size = outer * inner
    return hot((size, size), lambda m, r: r == (m % outer) * inner + m // outer)


def pick(band_images, pivots):
    band_dev, line_dev, cols = band_images.shape
    panels, panel = pivots.shape
    pivot_count = panels * panel
    shift = cols.bit_length() - 1
    chunks = 4
    step = band_dev // chunks
    rows = step * line_dev

    def kernel(x_ref, far_ref, held_ref, spec_ref, piv_ref, sems):
        def copy(i):
            part = pl.ds(i * step, step)
            return pltpu.make_async_copy(x_ref.at[part], held_ref.at[part], sems.at[i])

        indices = pltpu.make_async_copy(far_ref, piv_ref, sems.at[chunks])
        indices.start()
        for i in range(chunks):
            copy(i).start()
        indices.wait()
        flat = jnp.concatenate([piv_ref[i : i + 1, :] for i in range(panels)], axis=1).astype(f32)
        own = lax.broadcasted_iota(jnp.int32, (pivot_count, pivot_count), 0) == lax.broadcasted_iota(
            jnp.int32, (pivot_count, pivot_count), 1
        )
        flat = jnp.sum(jnp.where(own, flat, 0.0), axis=1, keepdims=True).astype(jnp.int32)
        column = flat & (cols - 1)
        inner = (flat >> shift) - lax.axis_index("row").astype(jnp.int32) * line_dev
        chosen = hot((pivot_count, cols), lambda k, c: c == column)
        lane = lax.broadcasted_iota(jnp.int32, (pivot_count, rows), 1)
        inside = lane % line_dev == inner
        fold = hot((step, rows), lambda b, r: r // line_dev == b)
        for i in range(chunks):
            copy(i).wait()
            part = held_ref[i * step : (i + 1) * step].reshape(rows, cols)
            found = jnp.where(inside, contract_last(chosen, part), 0.0).astype(bf16)
            spec_ref[i * step : (i + 1) * step, :] = contract_last(fold, found).astype(bf16)

    return pl.pallas_call(
        kernel,
        out_shape=(
            pltpu.VMEM(band_images.shape, bf16),
            pltpu.VMEM((band_dev, pivot_count), bf16),
        ),
        in_specs=[pl.BlockSpec(memory_space=pl.ANY), pl.BlockSpec(memory_space=pl.ANY)],
        scratch_shapes=[pltpu.VMEM(pivots.shape, pivots.dtype), pltpu.SemaphoreType.DMA((chunks + 1,))],
        name="pick",
    )(band_images, pivots)


def pack(band_images):
    band_dev, line_dev, cols = band_images.shape
    rows = band_dev * line_dev
    taken = LANES // band_dev
    groups = line_dev // taken
    wide = SUBLANES * line_dev
    sides = cols // wide

    def kernel(x_ref, out_ref, rows_ref, out_buf, sems):
        def give(j, q):
            part = (pl.ds(j * wide, wide), pl.ds(q * wide, wide))
            return pltpu.make_async_copy(out_buf.at[part], out_ref.at[part], sems.at[j, q])

        eye = hot((wide, wide), lambda m, r: m == r)
        mixed = swap_rows(SUBLANES, line_dev)
        for j in range(sides):
            side = slice(j * wide, (j + 1) * wide)
            for i in range(0, band_dev, 2 * SUBLANES):
                low, high = (
                    jnp.dot(
                        mixed,
                        x_ref[k : k + SUBLANES, :, side].reshape(wide, wide),
                        preferred_element_type=f32,
                    )
                    for k in (i, i + SUBLANES)
                )
                for line in range(line_dev):
                    start = ((line % groups) * taken + line // groups) * band_dev + i
                    at = slice(line * SUBLANES, (line + 1) * SUBLANES)
                    rows_ref[start : start + 2 * SUBLANES, side] = jnp.concatenate(
                        [low[at], high[at]], axis=0
                    ).astype(bf16)
            for q in range(rows // wide):
                part = slice(q * wide, (q + 1) * wide)
                out_buf[side, part] = contract_last(eye, rows_ref[part, side]).astype(bf16)
                give(j, q).start()
        for j in range(sides):
            for q in range(rows // wide):
                give(j, q).wait()

    return pl.pallas_call(
        kernel,
        out_shape=jax.ShapeDtypeStruct((cols, rows), bf16),
        in_specs=[pl.BlockSpec(memory_space=pltpu.VMEM)],
        out_specs=pl.BlockSpec(memory_space=pl.ANY),
        scratch_shapes=[
            pltpu.VMEM((rows, cols), bf16),
            pltpu.VMEM((cols, rows), bf16),
            pltpu.SemaphoreType.DMA((sides, rows // wide)),
        ],
        name="pack",
    )(pltpu.with_memory_space_constraint(band_images, pltpu.VMEM))


def finish(arrived, keep, gains, pix_count, row_count, band_dev, line_dev):
    _, narrow, _ = arrived.shape
    taken = LANES // band_dev
    groups = line_dev // taken
    lines = row_count * line_dev
    bands = pix_count * band_dev
    kept = gains.shape[0] // 2
    width = 4
    joined = bands // LANES
    pieces = narrow // width

    def swap(low, high, shift, mask):
        return (
            jnp.where(mask, low, pltpu.roll(high, shift, 1)),
            jnp.where(mask, pltpu.roll(low, LANES - shift, 1), high),
        )

    def kernel(a_ref, keep_ref, gain_ref, res_ref, coef_ref, x_ref, hold_ref, res_buf, coef_buf, sems):
        def give(i):
            part = pl.ds(i * width, width)
            return pltpu.make_async_copy(res_buf.at[part], res_ref.at[part], sems.at[i])

        last = pltpu.make_async_copy(coef_buf, coef_ref, sems.at[pieces])
        lane = lax.broadcasted_iota(jnp.int32, (SUBLANES, LANES), 1)
        half = groups * narrow
        mixed = hot(
            (2 * half, 2 * half),
            lambda m, r: r == (m // half) * half + (m % groups) * narrow + (m % half) // groups,
        )
        for r in range(row_count):
            for j in range(joined):
                sides = []
                for n in range(taken // 2):
                    tall = []
                    for s in range(2):
                        source = (j * taken + s * (taken // 2) + n) * row_count + r
                        tall += [a_ref[source, :, g * LANES : (g + 1) * LANES] for g in range(groups)]
                    sides.append(jnp.concatenate(tall, axis=0))
                turned = jnp.dot(mixed, jnp.concatenate(sides, axis=1), preferred_element_type=f32)
                for c in range(narrow):
                    v = []
                    for i in range(taken):
                        s, n = i // (taken // 2), i % (taken // 2)
                        start = (s * narrow + c) * groups
                        v.append(turned[start : start + groups, n * LANES : (n + 1) * LANES])
                    step = taken // 2
                    while step >= 1:
                        shift = step * band_dev
                        mask = (lane // shift) % 2 == 0
                        w = list(v)
                        for i in range(taken):
                            if (i // step) % 2 == 0:
                                w[i], w[i + step] = swap(v[i], v[i + step], shift, mask)
                        v = w
                        step //= 2
                    row = c * lines + r * line_dev
                    x_ref[row : row + line_dev, j * LANES : (j + 1) * LANES] = (
                        jnp.concatenate(v, axis=0).astype(bf16)
                    )
        for c in range(0, narrow, 2):
            found = contract_last(gain_ref[...], x_ref[c * lines : (c + 2) * lines, :])
            found = (found[:kept] + found[kept:]).astype(bf16)
            hold_ref[c] = found[:, :lines]
            hold_ref[c + 1] = found[:, lines:]
        turn = swap_rows(narrow, narrow)
        for k in range(0, kept, 2 * narrow):
            tall = [
                jnp.concatenate([hold_ref[c, q : q + narrow, :] for c in range(narrow)], axis=0)
                for q in (k, k + narrow)
            ]
            turned = jnp.dot(turn, jnp.concatenate(tall, axis=1), preferred_element_type=f32).astype(bf16)
            coef_buf[k : k + narrow] = turned[:, :lines].reshape(narrow, narrow, lines)
            coef_buf[k + narrow : k + 2 * narrow] = turned[:, lines:].reshape(narrow, narrow, lines)
        last.start()
        for p in range(pieces):
            pixels = x_ref[p * width * lines : (p + 1) * width * lines, :]
            both = jnp.dot(pixels, keep_ref[:bands], preferred_element_type=f32)
            both = both + jnp.dot(pixels, keep_ref[bands:], preferred_element_type=f32)
            res_buf[p * width : (p + 1) * width] = both.astype(bf16).reshape(width, lines, bands)
            give(p).start()
        last.wait()
        for p in range(pieces):
            give(p).wait()

    near = [pltpu.with_memory_space_constraint(v, pltpu.VMEM) for v in (arrived, keep, gains)]
    return pl.pallas_call(
        kernel,
        out_shape=(
            jax.ShapeDtypeStruct((narrow, lines, bands), bf16),
            jax.ShapeDtypeStruct((kept, narrow, lines), bf16),
        ),
        out_specs=(pl.BlockSpec(memory_space=pl.ANY), pl.BlockSpec(memory_space=pl.ANY)),
        scratch_shapes=[
            pltpu.VMEM((narrow * lines, bands), bf16),
            pltpu.VMEM((narrow, kept, lines), bf16),
            pltpu.VMEM((narrow, lines, bands), bf16),
            pltpu.VMEM((kept, narrow, lines), bf16),
            pltpu.SemaphoreType.DMA((pieces + 1,)),
        ],
        name="finish",
    )(*near)


def factor(spectra):
    bands, count = spectra.shape
    half = count // 2

    def kernel(s_ref, keep_ref, gain_ref):
        s = s_ref[...].astype(f32)
        st = s.T
        gram = jnp.dot(st, s, precision=highest, preferred_element_type=f32)
        row = lax.broadcasted_iota(jnp.int32, (count, 2 * count), 0)
        lane = lax.broadcasted_iota(jnp.int32, (count, 2 * count), 1)
        both = jnp.concatenate([gram, jnp.where(lane == row, 1.0, 0.0)[:, :count]], axis=1)
        done = []
        for j in range(count):
            base = j // SUBLANES * SUBLANES
            scale = 1.0 / jnp.sqrt(both[j - base : j - base + 1, j : j + 1])
            top = both[j - base : j - base + 1, :] * scale
            done.append(top[:, count:])
            if (j + 1) % SUBLANES == 0:
                both = both[SUBLANES:]
            if j + 1 < count:
                column = both[:, j : j + 1] * scale
                both = both - column * top
        inverse = jnp.concatenate(done, axis=0)
        basis = jnp.dot(inverse, st, precision=highest, preferred_element_type=f32)
        tall = basis.T
        cross = lax.dot_general(
            basis[:half], basis[half:], (((1,), (1,)), ((), ())), precision=highest, preferred_element_type=f32
        )
        second = tall[:, half:] - jnp.dot(tall[:, :half], cross, precision=highest, preferred_element_type=f32)
        gains = jnp.concatenate([tall[:, :half], second], axis=1)
        keep = jnp.where(
            lax.broadcasted_iota(jnp.int32, (bands, bands), 0)
            == lax.broadcasted_iota(jnp.int32, (bands, bands), 1),
            1.0,
            0.0,
        ) - jnp.dot(gains, basis, precision=highest, preferred_element_type=f32)
        gains = gains.T
        for ref, value, size in ((keep_ref, keep, bands), (gain_ref, gains, count)):
            high = value.astype(bf16)
            ref[:size] = high
            ref[size:] = (value - high.astype(f32)).astype(bf16)

    return pl.pallas_call(
        kernel,
        out_shape=(
            pltpu.VMEM((2 * bands, bands), bf16),
            pltpu.VMEM((2 * count, bands), bf16),
        ),
        name="factor",
    )(spectra)


def exchange(x, axis, k):
    count = lax.axis_size(axis)
    return lax.ppermute(x, axis, [(i, i ^ k) for i in range(count)])


def orthonormal(spectra):
    gram = jnp.dot(spectra, spectra.T, precision=highest)
    factor = jnp.linalg.cholesky(gram)
    return jax.scipy.linalg.solve_triangular(factor, spectra, lower=True)


def project(block, basis):
    count = basis.shape[0] // 2
    first = basis[:count]
    second = basis[count:]
    coef_one = jnp.einsum("clb,kb->kcl", block, first, precision=highest)
    remain = block - jnp.einsum("kcl,kb->clb", coef_one, first, precision=highest)
    coef_two = jnp.einsum("clb,kb->kcl", remain, second, precision=highest)
    remain = remain - jnp.einsum("kcl,kb->clb", coef_two, second, precision=highest)
    return (
        remain.astype(bf16),
        jnp.concatenate([coef_one, coef_two], axis=0).astype(bf16),
    )


def plain(band_images, line_index, column, pix_count, row_count, narrow):
    band_dev, line_dev, cols_all = band_images.shape
    offset = line_index - lax.axis_index("row") * line_dev
    inside = (offset >= 0) & (offset < line_dev)
    position = jnp.clip(offset, 0, line_dev - 1) * cols_all + column
    picked = jnp.take(band_images.reshape(band_dev, line_dev * cols_all), position, axis=1)
    picked = jnp.where(inside[None, :], picked, jnp.zeros_like(picked))
    stacked = lax.all_gather(picked, "pix", axis=0, tiled=True)
    spectra = lax.psum(stacked.astype(f32).astype(bf16), "row").astype(f32)
    basis = orthonormal(spectra.T)
    shaped = band_images.reshape(band_dev, line_dev, pix_count, row_count, narrow)
    arrived = lax.all_to_all(
        lax.all_to_all(shaped, "pix", split_axis=2, concat_axis=0, tiled=True),
        "row",
        split_axis=3,
        concat_axis=1,
        tiled=True,
    )
    block = (
        arrived.reshape(arrived.shape[0], arrived.shape[1], narrow)
        .transpose(2, 1, 0)
        .astype(f32)
    )
    return project(block, basis)


def shards(band_images, pivots):
    band_dev, line_dev, cols_all = band_images.shape
    pix_count = lax.axis_size("pix")
    row_count = lax.axis_size("row")
    part_count = pix_count * row_count
    narrow = cols_all // part_count
    flat_pivots = pivots.reshape(-1)
    pivot_count = flat_pivots.shape[0]
    line_index = flat_pivots // cols_all
    column = flat_pivots % cols_all
    lines = row_count * line_dev
    bands = pix_count * band_dev
    taken = LANES // band_dev
    fits = (
        taken * band_dev == LANES
        and taken in (2, 4)
        and line_dev == SUBLANES * taken
        and narrow == 16
        and cols_all % (SUBLANES * line_dev) == 0
        and lines == LANES
        and 2 * pivot_count == LANES
        and bands % LANES == 0
        and cols_all & (cols_all - 1) == 0
        and pix_count & (pix_count - 1) == 0
        and row_count & (row_count - 1) == 0
    )
    if not fits:
        return plain(band_images, line_index, column, pix_count, row_count, narrow)
    held, picked = pick(band_images, pivots)
    found = picked
    for k in range(row_count.bit_length() - 1):
        found = found + exchange(found, "row", 1 << k)
    packed = pack(held).reshape(part_count, narrow, line_dev * band_dev)
    arrived = lax.all_to_all(packed, AXES, 0, 0, tiled=True)
    for k in range(pix_count.bit_length() - 1):
        other = exchange(found, "pix", 1 << k)
        after = (lax.axis_index("pix") >> k) % 2 == 1
        found = jnp.where(after, jnp.concatenate([other, found], axis=0), jnp.concatenate([found, other], axis=0))
    keep, gains = factor(found)
    return finish(arrived, keep, gains, pix_count, row_count, band_dev, line_dev)


def solution(mesh):
    placed = (P("pix", "row", None), P())
    return jax.shard_map(
        shards,
        mesh=mesh,
        in_specs=placed,
        out_specs=(P(AXES, None, None), P(None, AXES, None)),
        check_vma=False,
    )
```

profile of v0, /device:TPU:0, one launch (start us, length us, event | category | flops | bytes accessed | tf_op | source)
XLA Modules:
  0.0 59.7 jit_solution(17645047474808960380)
XLA Ops:
  0.6 2.6 %pick.1 = (bf16[32,32,512]{2,1,0:T(8,128)(2,1)S(1)}, bf16[32,64]{1,0:T(8,128)(2,1)S(1)}) custom-call(bf16[32,32,512]{2,1,0:T(8,128)(2,1)} %x_ref.1, s32[2,32]{1,0:T(2,128)} %far_ref.1), custom_call_target="tpu_custom_call" | custom-call | tf_op jit(solution)/shard_map/pick/pallas_call | solution.py:68
  3.2 1.8 %pack.1 = bf16[512,1024]{1,0:T(8,128)(2,1)} custom-call(bf16[32,32,512]{2,1,0:T(8,128)(2,1)S(1)} %get-tuple-element.6.x_ref), custom_call_target="tpu_custom_call" | custom-call | tf_op jit(solution)/shard_map/pack/pallas_call | solution.py:120
  5.0 7.3 %all-to-all-start = ((bf16[32,16,1024]{2,1,0:T(8,128)(2,1)}), bf16[32,16,1024]{2,1,0:T(8,128)(2,1)S(1)}, u32[]{:S(2)}, u32[]{:S(2)}) async-start(bf16[32,16,1024]{2,1,0:T(8,128)(2,1)} %bitcast.1), calls=%async_computation | async-start | bytes 2097152 | tf_op jit(solution)/shard_map/all_to_all | solution.py:373
  12.4 1.8 %collective-permute-start = (bf16[32,64]{1,0:T(8,128)(2,1)S(1)}, bf16[32,64]{1,0:T(8,128)(2,1)S(1)}, u32[]{:S(2)}, u32[]{:S(2)}) collective-permute-start(bf16[32,64]{1,0:T(8,128)(2,1)S(1)} %get-tuple-element.7), channel_id=1, source_target_pairs={{0,1},{1,0},{2,3},{3,2},{4,5},{5,4},{6,7},{7,6},{8,9},{9,8},{10,11... | collective-permute-start | bytes 12296 | tf_op jit(solution)/shard_map/ppermute | solution.py:291
  14.2 16.0 %collective-permute-done = bf16[32,64]{1,0:T(8,128)(2,1)S(1)} collective-permute-done((bf16[32,64]{1,0:T(8,128)(2,1)S(1)}, bf16[32,64]{1,0:T(8,128)(2,1)S(1)}, u32[]{:S(2)}, u32[]{:S(2)}) %collective-permute-start) | collective-permute-done | bytes 4128 | tf_op jit(solution)/shard_map/ppermute | solution.py:291
  30.2 4.4 %collective-permute-start.1 = (bf16[32,64]{1,0:T(8,128)(2,1)S(1)}, bf16[32,64]{1,0:T(8,128)(2,1)S(1)}, u32[]{:S(2)}, u32[]{:S(2)}) collective-permute-start(bf16[32,64]{1,0:T(8,128)(2,1)S(1)} %add.19), channel_id=1, source_target_pairs={{0,2},{1,3},{2,0},{3,1},{4,6},{5,7},{6,4},{7,5},{8,10},{9,11},{10,... | collective-permute-start | bytes 12296 | tf_op jit(solution)/shard_map/ppermute | solution.py:291
  34.7 4.3 %collective-permute-done.1 = bf16[32,64]{1,0:T(8,128)(2,1)S(1)} collective-permute-done((bf16[32,64]{1,0:T(8,128)(2,1)S(1)}, bf16[32,64]{1,0:T(8,128)(2,1)S(1)}, u32[]{:S(2)}, u32[]{:S(2)}) %collective-permute-start.1) | collective-permute-done | bytes 4128 | tf_op jit(solution)/shard_map/ppermute | solution.py:291
  38.9 0.0 collective-permute-start.2
  39.0 1.2 %collective-permute-done.2 = bf16[32,64]{1,0:T(8,128)(2,1)S(1)} collective-permute-done((bf16[32,64]{1,0:T(8,128)(2,1)S(1)}, bf16[32,64]{1,0:T(8,128)(2,1)S(1)}, u32[]{:S(2)}, u32[]{:S(2)}) %collective-permute-start.2) | collective-permute-done | bytes 4128 | tf_op jit(solution)/shard_map/ppermute | solution.py:291
  40.1 1.5 %collective-permute-start.3 = (bf16[64,64]{1,0:T(8,128)(2,1)S(1)}, bf16[64,64]{1,0:T(8,128)(2,1)S(1)}, u32[]{:S(2)}, u32[]{:S(2)}) collective-permute-start(bf16[64,64]{1,0:T(8,128)(2,1)S(1)} %maximum_select_fusion.2), channel_id=1, source_target_pairs={{0,8},{4,12},{8,0},{12,4},{16,24},{20,28},{24,16},{28,20},{1,9},{5... | collective-permute-start | bytes 24584 | tf_op jit(solution)/shard_map/ppermute | solution.py:291
  41.7 2.3 %collective-permute-done.3 = bf16[64,64]{1,0:T(8,128)(2,1)S(1)} collective-permute-done((bf16[64,64]{1,0:T(8,128)(2,1)S(1)}, bf16[64,64]{1,0:T(8,128)(2,1)S(1)}, u32[]{:S(2)}, u32[]{:S(2)}) %collective-permute-start.3) | collective-permute-done | bytes 8224 | tf_op jit(solution)/shard_map/ppermute | solution.py:291
  43.9 1.5 %collective-permute-start.4 = (bf16[128,64]{1,0:T(8,128)(2,1)S(1)}, bf16[128,64]{1,0:T(8,128)(2,1)S(1)}, u32[]{:S(2)}, u32[]{:S(2)}) collective-permute-start(bf16[128,64]{1,0:T(8,128)(2,1)S(1)} %maximum_select_fusion.1), channel_id=1, source_target_pairs={{0,16},{4,20},{8,24},{12,28},{16,0},{20,4},{24,8},{28,12},{1,17},{... | collective-permute-start | bytes 49160 | tf_op jit(solution)/shard_map/ppermute | solution.py:291
  45.5 2.4 %collective-permute-done.4 = bf16[128,64]{1,0:T(8,128)(2,1)S(1)} collective-permute-done((bf16[128,64]{1,0:T(8,128)(2,1)S(1)}, bf16[128,64]{1,0:T(8,128)(2,1)S(1)}, u32[]{:S(2)}, u32[]{:S(2)}) %collective-permute-start.4) | collective-permute-done | bytes 16416 | tf_op jit(solution)/shard_map/ppermute | solution.py:291
  47.9 0.7 %maximum_select_fusion.s_ref = bf16[256,64]{1,0:T(8,128)(2,1)} fusion(bf16[128,64]{1,0:T(8,128)(2,1)S(1)} %maximum_select_fusion.1, bf16[128,64]{1,0:T(8,128)(2,1)S(1)} %collective-permute-done.4, pred[]{:T(512)S(6)} %eq.13), kind=kLoop, calls=%fused_computation | loop fusion | flops 147456 | bytes 65537 | tf_op jit(solution)/shard_map/jit(_where)/select_n | solution.py:377
  48.6 8.4 %factor.1 = (bf16[512,256]{1,0:T(8,128)(2,1)S(1)}, bf16[128,256]{1,0:T(8,128)(2,1)S(1)}) custom-call(bf16[256,64]{1,0:T(8,128)(2,1)} %maximum_select_fusion.s_ref), custom_call_target="tpu_custom_call" | custom-call | tf_op jit(solution)/shard_map/factor/pallas_call | solution.py:279
  57.0 0.0 all-to-all-done.a_ref
  57.0 2.8 %finish.1 = (bf16[16,128,256]{2,1,0:T(8,128)(2,1)}, bf16[64,16,128]{2,1,0:T(8,128)(2,1)}) custom-call(bf16[32,16,1024]{2,1,0:T(8,128)(2,1)S(1)} %all-to-all-done.a_ref, bf16[512,256]{1,0:T(8,128)(2,1)S(1)} %get-tuple-element.8.keep_ref, bf16[128,256]{1,0:T(8,128)(2,1)S(1)} %get-tuple-element.9.gain_ref), custom_call_target="tpu_custom_call" | custom-call | tf_op jit(solution)/shard_map/finish/pallas_call | solution.py:219
  (4 shorter events, 0.0 us)
Async XLA Ops:
  5.0 52.0 %all-to-all-start = ((bf16[32,16,1024]{2,1,0:T(8,128)(2,1)}), bf16[32,16,1024]{2,1,0:T(8,128)(2,1)S(1)}, u32[]{:S(2)}, u32[]{:S(2)}) async-start(bf16[32,16,1024]{2,1,0:T(8,128)(2,1)} %bitcast.1), calls=%async_computation | async-start | bytes 2097152 | tf_op jit(solution)/shard_map/all_to_all | solution.py:373
  12.4 17.8 %collective-permute-start = (bf16[32,64]{1,0:T(8,128)(2,1)S(1)}, bf16[32,64]{1,0:T(8,128)(2,1)S(1)}, u32[]{:S(2)}, u32[]{:S(2)}) collective-permute-start(bf16[32,64]{1,0:T(8,128)(2,1)S(1)} %get-tuple-element.7), channel_id=1, source_target_pairs={{0,1},{1,0},{2,3},{3,2},{4,5},{5,4},{6,7},{7,6},{8,9},{9,8},{10,11... | collective-permute-start | bytes 12296 | tf_op jit(solution)/shard_map/ppermute | solution.py:291
  30.2 8.7 %collective-permute-start.1 = (bf16[32,64]{1,0:T(8,128)(2,1)S(1)}, bf16[32,64]{1,0:T(8,128)(2,1)S(1)}, u32[]{:S(2)}, u32[]{:S(2)}) collective-permute-start(bf16[32,64]{1,0:T(8,128)(2,1)S(1)} %add.19), channel_id=1, source_target_pairs={{0,2},{1,3},{2,0},{3,1},{4,6},{5,7},{6,4},{7,5},{8,10},{9,11},{10,... | collective-permute-start | bytes 12296 | tf_op jit(solution)/shard_map/ppermute | solution.py:291
  38.9 1.2 %collective-permute-start.2 = (bf16[32,64]{1,0:T(8,128)(2,1)S(1)}, bf16[32,64]{1,0:T(8,128)(2,1)S(1)}, u32[]{:S(2)}, u32[]{:S(2)}) collective-permute-start(bf16[32,64]{1,0:T(8,128)(2,1)S(1)} %add.20), channel_id=1, source_target_pairs={{0,4},{4,0},{8,12},{12,8},{16,20},{20,16},{24,28},{28,24},{1,5},{5... | collective-permute-start | bytes 12296 | tf_op jit(solution)/shard_map/ppermute | solution.py:291
  40.1 3.8 %collective-permute-start.3 = (bf16[64,64]{1,0:T(8,128)(2,1)S(1)}, bf16[64,64]{1,0:T(8,128)(2,1)S(1)}, u32[]{:S(2)}, u32[]{:S(2)}) collective-permute-start(bf16[64,64]{1,0:T(8,128)(2,1)S(1)} %maximum_select_fusion.2), channel_id=1, source_target_pairs={{0,8},{4,12},{8,0},{12,4},{16,24},{20,28},{24,16},{28,20},{1,9},{5... | collective-permute-start | bytes 24584 | tf_op jit(solution)/shard_map/ppermute | solution.py:291
  43.9 4.0 %collective-permute-start.4 = (bf16[128,64]{1,0:T(8,128)(2,1)S(1)}, bf16[128,64]{1,0:T(8,128)(2,1)S(1)}, u32[]{:S(2)}, u32[]{:S(2)}) collective-permute-start(bf16[128,64]{1,0:T(8,128)(2,1)S(1)} %maximum_select_fusion.1), channel_id=1, source_target_pairs={{0,16},{4,20},{8,24},{12,28},{16,0},{20,4},{24,8},{28,12},{1,17},{... | collective-permute-start | bytes 49160 | tf_op jit(solution)/shard_map/ppermute | solution.py:291
where the time goes:
time: 60 us; the launch traced here: 59.7 us
  waiting for transfers between devices  26.1 us (44%)
  starting transfers between devices  16.7 us (28%)
  Pallas kernels  15.5 us (26%)
  between operations  0.7 us (1%)
  other arithmetic  0.68 us (1%)
    ppermute x5, waiting for transfers between devices, exchange(): return lax.ppermute(x, axis, [(i, i ^ k) for i in range(count)])  26.1 us
    ppermute x5, starting transfers between devices, exchange(): return lax.ppermute(x, axis, [(i, i ^ k) for i in range(count)])  9.37 us
    pallas_call x1, Pallas kernels, factor(): pl.pallas_call(kernel, out_shape=(pltpu.VMEM((2 * bands, bands), bf16), p...  8.4 us
    all_to_all x1, starting transfers between devices, shards(): arrived = lax.all_to_all(packed, AXES, 0, 0, tiled=True)  7.33 us
    pallas_call x1, Pallas kernels, finish(): pl.pallas_call(kernel, out_shape=(jax.ShapeDtypeStruct((narrow, lines, ba...  2.75 us
    pallas_call x1, Pallas kernels, pick(): pl.pallas_call(kernel, out_shape=(pltpu.VMEM(band_images.shape, bf16), pl...  2.55 us
    pallas_call x1, Pallas kernels, pack(): pl.pallas_call(kernel, out_shape=jax.ShapeDtypeStruct((cols, rows), bf16)...  1.84 us
  transfers between devices with their start and end apart: 6, of which 5 were waited for; matrix products, arithmetic and copies ran while one was open for 1% of the time, Pallas kernels for 14%

commit v1 on v0

v1 whole, which is shorter than its diff:
```python
import jax
import jax.numpy as jnp
from jax import lax
from jax.experimental import pallas as pl
from jax.experimental.pallas import tpu as pltpu
from jax.sharding import PartitionSpec as P


highest = lax.Precision.HIGHEST
f32 = jnp.float32
bf16 = jnp.bfloat16
LANES = 128
SUBLANES = 8
TILE = 16
AXES = ("pix", "row")


def contract_last(a, b):
    return lax.dot_general(a, b, (((1,), (1,)), ((), ())), preferred_element_type=f32)


def hot(shape, test):
    row = lax.broadcasted_iota(jnp.int32, shape, 0)
    column = lax.broadcasted_iota(jnp.int32, shape, 1)
    return test(row, column).astype(f32).astype(bf16)


def swap_rows(outer, inner):
    size = outer * inner
    return hot((size, size), lambda m, r: r == (m % outer) * inner + m // outer)


def pick(band_images, pivots):
    band_dev, line_dev, cols = band_images.shape
    panels, panel = pivots.shape
    pivot_count = panels * panel
    taken = LANES // band_dev
    groups = line_dev // taken
    shift = cols.bit_length() - 1
    chunks = band_dev // TILE
    rows = TILE * line_dev
    wide = TILE * TILE

    def kernel(x_ref, far_ref, rows_ref, spec_ref, plan_ref, held_ref, piv_ref, sems):
        def copy(i):
            part = pl.ds(i * TILE, TILE)
            return pltpu.make_async_copy(x_ref.at[part], held_ref.at[part], sems.at[i])

        indices = pltpu.make_async_copy(far_ref, piv_ref, sems.at[chunks])
        indices.start()
        for i in range(chunks):
            copy(i).start()
        mixed = swap_rows(TILE, TILE)
        plan_ref[:wide] = mixed
        plan_ref[wide : 2 * wide] = hot((wide, wide), lambda m, r: m == r)
        tall = groups * TILE
        plan_ref[2 * wide :] = hot(
            (wide, wide), lambda m, r: r == (m // tall) * tall + (m % groups) * TILE + (m % tall) // groups
        )
        indices.wait()
        flat = jnp.concatenate([piv_ref[i : i + 1, :] for i in range(panels)], axis=1).astype(f32)
        own = lax.broadcasted_iota(jnp.int32, (pivot_count, pivot_count), 0) == lax.broadcasted_iota(
            jnp.int32, (pivot_count, pivot_count), 1
        )
        flat = jnp.sum(jnp.where(own, flat, 0.0), axis=1, keepdims=True).astype(jnp.int32)
        column = flat & (cols - 1)
        inner = (flat >> shift) - lax.axis_index("row").astype(jnp.int32) * line_dev
        chosen = hot((pivot_count, cols), lambda k, c: c == column)
        lane = lax.broadcasted_iota(jnp.int32, (pivot_count, rows), 1)
        inside = lane % line_dev == inner
        fold = hot((TILE, rows), lambda b, r: r // line_dev == b)
        for i in range(chunks):
            copy(i).wait()
            bands = slice(i * TILE, (i + 1) * TILE)
            found = contract_last(chosen, held_ref[bands].reshape(rows, cols))
            found = jnp.where(inside, found, 0.0).astype(bf16)
            spec_ref[bands, :] = contract_last(fold, found).astype(bf16)
            for h in range(line_dev // TILE):
                block = held_ref[bands, h * TILE : (h + 1) * TILE, :].reshape(wide, cols)
                block = jnp.dot(mixed, block, preferred_element_type=f32).astype(bf16)
                for k in range(TILE):
                    line = h * TILE + k
                    start = ((line % groups) * taken + line // groups) * band_dev + i * TILE
                    rows_ref[start : start + TILE, :] = block[k * TILE : (k + 1) * TILE]

    return pl.pallas_call(
        kernel,
        out_shape=(
            pltpu.VMEM((line_dev * band_dev, cols), bf16),
            pltpu.VMEM((band_dev, pivot_count), bf16),
            pltpu.VMEM((3 * wide, wide), bf16),
        ),
        in_specs=[pl.BlockSpec(memory_space=pl.ANY), pl.BlockSpec(memory_space=pl.ANY)],
        scratch_shapes=[
            pltpu.VMEM(band_images.shape, bf16),
            pltpu.VMEM(pivots.shape, pivots.dtype),
            pltpu.SemaphoreType.DMA((chunks + 1,)),
        ],
        name="pick",
    )(band_images, pivots)


def near(*arrays):
    return [pltpu.with_memory_space_constraint(v, pltpu.VMEM) for v in arrays]


def pack(ordered, plans):
    rows, cols = ordered.shape
    wide = plans.shape[1]
    sides = cols // wide

    def kernel(x_ref, plan_ref, out_ref, out_buf, sems):
        def give(j, q):
            part = (pl.ds(j * wide, wide), pl.ds(q * wide, wide))
            return pltpu.make_async_copy(out_buf.at[part], out_ref.at[part], sems.at[j, q])

        for j in range(sides):
            for q in range(rows // wide):
                side = slice(j * wide, (j + 1) * wide)
                part = slice(q * wide, (q + 1) * wide)
                out_buf[side, part] = contract_last(plan_ref[wide : 2 * wide], x_ref[part, side]).astype(bf16)
                give(j, q).start()
        for j in range(sides):
            for q in range(rows // wide):
                give(j, q).wait()

    return pl.pallas_call(
        kernel,
        out_shape=jax.ShapeDtypeStruct((cols, rows), bf16),
        out_specs=pl.BlockSpec(memory_space=pl.ANY),
        scratch_shapes=[
            pltpu.VMEM((cols, rows), bf16),
            pltpu.SemaphoreType.DMA((sides, rows // wide)),
        ],
        name="pack",
    )(*near(ordered, plans))


def finish(arrived, keep, gains, plans, row_count, band_dev, line_dev):
    sources, narrow, _ = arrived.shape
    taken = LANES // band_dev
    groups = line_dev // taken
    lines = row_count * line_dev
    bands = sources // row_count * band_dev
    kept = gains.shape[0] // 2
    width = 4
    joined = bands // LANES
    pieces = narrow // width

    def swap(low, high, shift, mask):
        return (
            jnp.where(mask, low, pltpu.roll(high, shift, 1)),
            jnp.where(mask, pltpu.roll(low, LANES - shift, 1), high),
        )

    def kernel(a_ref, keep_ref, gain_ref, plan_ref, res_ref, coef_ref, x_ref, hold_ref, res_buf, coef_buf, sems):
        def give(i):
            at = pl.ds(i * width, width)
            return pltpu.make_async_copy(res_buf.at[at], res_ref.at[at], sems.at[i])

        last = pltpu.make_async_copy(coef_buf, coef_ref, sems.at[pieces])
        lane = lax.broadcasted_iota(jnp.int32, (groups, LANES), 1)
        size = plan_ref.shape[1]
        for r in range(row_count):
            for j in range(joined):
                sides = []
                for n in range(taken // 2):
                    tall = []
                    for s in range(2):
                        source = (j * taken + s * (taken // 2) + n) * row_count + r
                        tall += [a_ref[source, :, g * LANES : (g + 1) * LANES] for g in range(groups)]
                    sides.append(jnp.concatenate(tall, axis=0))
                turned = jnp.dot(
                    plan_ref[2 * size :], jnp.concatenate(sides, axis=1), preferred_element_type=f32
                )
                for c in range(narrow):
                    v = []
                    for i in range(taken):
                        s, n = i // (taken // 2), i % (taken // 2)
                        start = (s * narrow + c) * groups
                        v.append(turned[start : start + groups, n * LANES : (n + 1) * LANES])
                    step = taken // 2
                    while step >= 1:
                        shift = step * band_dev
                        mask = (lane // shift) % 2 == 0
                        w = list(v)
                        for i in range(taken):
                            if (i // step) % 2 == 0:
                                w[i], w[i + step] = swap(v[i], v[i + step], shift, mask)
                        v = w
                        step //= 2
                    row = c * lines + r * line_dev
                    x_ref[row : row + line_dev, j * LANES : (j + 1) * LANES] = (
                        jnp.concatenate(v, axis=0).astype(bf16)
                    )
        for c in range(0, narrow, 2):
            found = contract_last(gain_ref[...], x_ref[c * lines : (c + 2) * lines, :])
            found = (found[:kept] + found[kept:]).astype(bf16)
            hold_ref[c] = found[:, :lines]
            hold_ref[c + 1] = found[:, lines:]
        for k in range(0, kept, 2 * narrow):
            tall = [
                jnp.concatenate([hold_ref[c, q : q + narrow, :] for c in range(narrow)], axis=0)
                for q in (k, k + narrow)
            ]
            turned = jnp.dot(
                plan_ref[:size], jnp.concatenate(tall, axis=1), preferred_element_type=f32
            ).astype(bf16)
            coef_buf[k : k + narrow] = turned[:, :lines].reshape(narrow, narrow, lines)
            coef_buf[k + narrow : k + 2 * narrow] = turned[:, lines:].reshape(narrow, narrow, lines)
        last.start()
        for p in range(pieces):
            pixels = x_ref[p * width * lines : (p + 1) * width * lines, :]
            both = jnp.dot(pixels, keep_ref[:bands], preferred_element_type=f32)
            both = both + jnp.dot(pixels, keep_ref[bands:], preferred_element_type=f32)
            res_buf[p * width : (p + 1) * width] = both.astype(bf16).reshape(width, lines, bands)
            give(p).start()
        last.wait()
        for p in range(pieces):
            give(p).wait()

    return pl.pallas_call(
        kernel,
        out_shape=(
            jax.ShapeDtypeStruct((narrow, lines, bands), bf16),
            jax.ShapeDtypeStruct((kept, narrow, lines), bf16),
        ),
        out_specs=(pl.BlockSpec(memory_space=pl.ANY), pl.BlockSpec(memory_space=pl.ANY)),
        scratch_shapes=[
            pltpu.VMEM((narrow * lines, bands), bf16),
            pltpu.VMEM((narrow, kept, lines), bf16),
            pltpu.VMEM((narrow, lines, bands), bf16),
            pltpu.VMEM((kept, narrow, lines), bf16),
            pltpu.SemaphoreType.DMA((pieces + 1,)),
        ],
        name="finish",
    )(*near(arrived, keep, gains, plans))


def parts_of(a, count):
    out = []
    for _ in range(count):
        high = a.astype(bf16)
        out.append(high)
        a = a - high.astype(f32)
    return out


def factor(spectra, parts):
    bands, count = spectra.shape
    half = count // 2
    width = 2 * count

    def row_of(tile, i):
        return jnp.broadcast_to(tile[i : i + 1, :], tile.shape)

    def lane_of(tile, i):
        return jnp.broadcast_to(tile[:, i : i + 1], tile.shape)

    def inverse_of(gram):
        row = lax.broadcasted_iota(jnp.int32, (count, count), 0)
        lane = lax.broadcasted_iota(jnp.int32, (count, count), 1)
        both = jnp.concatenate([gram, jnp.where(lane == row, 1.0, 0.0)], axis=1)
        tiles = [both[i : i + SUBLANES] for i in range(0, count, SUBLANES)]
        place = lax.broadcasted_iota(jnp.int32, (SUBLANES, width), 0)
        done = []
        for first in range(len(tiles)):
            live = range(first, len(tiles))
            columns = [
                {i: lane_of(tiles[i], first * SUBLANES + k) for i in live} for k in range(SUBLANES)
            ]
            kept = tiles[first]
            for k in range(SUBLANES):
                scale = lax.rsqrt(row_of(columns[k][first], k))
                column = {i: columns[k][i] * scale for i in live}
                top = row_of(tiles[first], k) * scale
                kept = jnp.where(place == k, top, kept)
                for q in range(k + 1, SUBLANES):
                    other = row_of(column[first], q)
                    for i in live:
                        columns[q][i] = columns[q][i] - column[i] * other
                for i in live:
                    tiles[i] = tiles[i] - column[i] * top
            done.append(kept)
        return jnp.concatenate(done, axis=0)[:, count:]

    def kernel(s_ref, keep_ref, gain_ref):
        me = lax.axis_index("pix").astype(jnp.int32)
        own = bands // parts
        s = jnp.concatenate(
            [s_ref[pl.ds(pl.multiple_of((me ^ k) * own, own), own), :] for k in range(parts)], axis=0
        )
        st = contract_last(hot((count, count), lambda k, q: k == q), s).astype(bf16)
        pieces = parts_of(inverse_of(contract_last(st, st)), 3)
        basis = sum(contract_last(p, s) for p in pieces[::-1])
        tall = sum(contract_last(s, p) for p in pieces[::-1])
        high, low = parts_of(basis, 2)
        one, two = slice(0, half), slice(half, count)

        def products(a, b):
            return contract_last(high[a], high[b]) + (contract_last(high[a], low[b]) + contract_last(low[a], high[b]))

        across = products(one, two)
        back = products(two, one)

        def times(a, b):
            a_high, a_low = parts_of(a, 2)
            b_high, b_low = parts_of(b, 2)
            return jnp.dot(
                jnp.concatenate([a_high, a_low, a_high], axis=1),
                jnp.concatenate([b_high, b_high, b_low], axis=0),
                preferred_element_type=f32,
            )

        gains = jnp.concatenate([basis[one], basis[two] - times(back, basis[one])], axis=0)
        other = jnp.concatenate([tall[:, one], tall[:, two] - times(tall[:, one], across)], axis=1)
        eye = jnp.where(
            lax.broadcasted_iota(jnp.int32, (bands, bands), 0)
            == lax.broadcasted_iota(jnp.int32, (bands, bands), 1),
            1.0,
            0.0,
        )
        keep = eye - times(other, basis)
        for ref, value, size in ((keep_ref, keep, bands), (gain_ref, gains, count)):
            ref[:size], ref[size:] = parts_of(value, 2)

    return pl.pallas_call(
        kernel,
        out_shape=(
            pltpu.VMEM((2 * bands, bands), bf16),
            pltpu.VMEM((2 * count, bands), bf16),
        ),
        name="factor",
    )(*near(spectra))


def exchange(x, axis, k):
    count = lax.axis_size(axis)
    return lax.ppermute(x, axis, [(i, i ^ k) for i in range(count)])


def orthonormal(spectra):
    gram = jnp.dot(spectra, spectra.T, precision=highest)
    factor = jnp.linalg.cholesky(gram)
    return jax.scipy.linalg.solve_triangular(factor, spectra, lower=True)


def project(block, basis):
    count = basis.shape[0] // 2
    first = basis[:count]
    second = basis[count:]
    coef_one = jnp.einsum("clb,kb->kcl", block, first, precision=highest)
    remain = block - jnp.einsum("kcl,kb->clb", coef_one, first, precision=highest)
    coef_two = jnp.einsum("clb,kb->kcl", remain, second, precision=highest)
    remain = remain - jnp.einsum("kcl,kb->clb", coef_two, second, precision=highest)
    return (
        remain.astype(bf16),
        jnp.concatenate([coef_one, coef_two], axis=0).astype(bf16),
    )


def plain(band_images, line_index, column, pix_count, row_count, narrow):
    band_dev, line_dev, cols_all = band_images.shape
    offset = line_index - lax.axis_index("row") * line_dev
    inside = (offset >= 0) & (offset < line_dev)
    position = jnp.clip(offset, 0, line_dev - 1) * cols_all + column
    picked = jnp.take(band_images.reshape(band_dev, line_dev * cols_all), position, axis=1)
    picked = jnp.where(inside[None, :], picked, jnp.zeros_like(picked))
    stacked = lax.all_gather(picked, "pix", axis=0, tiled=True)
    spectra = lax.psum(stacked.astype(f32).astype(bf16), "row").astype(f32)
    basis = orthonormal(spectra.T)
    shaped = band_images.reshape(band_dev, line_dev, pix_count, row_count, narrow)
    arrived = lax.all_to_all(
        lax.all_to_all(shaped, "pix", split_axis=2, concat_axis=0, tiled=True),
        "row",
        split_axis=3,
        concat_axis=1,
        tiled=True,
    )
    block = (
        arrived.reshape(arrived.shape[0], arrived.shape[1], narrow)
        .transpose(2, 1, 0)
        .astype(f32)
    )
    return project(block, basis)


def shards(band_images, pivots):
    band_dev, line_dev, cols_all = band_images.shape
    pix_count = lax.axis_size("pix")
    row_count = lax.axis_size("row")
    part_count = pix_count * row_count
    narrow = cols_all // part_count
    flat_pivots = pivots.reshape(-1)
    pivot_count = flat_pivots.shape[0]
    line_index = flat_pivots // cols_all
    column = flat_pivots % cols_all
    lines = row_count * line_dev
    bands = pix_count * band_dev
    taken = LANES // band_dev
    fits = (
        taken in (2, 4)
        and taken * band_dev == LANES
        and line_dev == SUBLANES * taken
        and band_dev % TILE == 0
        and line_dev % TILE == 0
        and narrow == TILE
        and lines == LANES
        and bands % LANES == 0
        and 2 * pivot_count == LANES
        and cols_all % (TILE * TILE) == 0
        and cols_all & (cols_all - 1) == 0
        and pix_count & (pix_count - 1) == 0
        and row_count & (row_count - 1) == 0
    )
    if not fits:
        return plain(band_images, line_index, column, pix_count, row_count, narrow)
    ordered, picked, plans = pick(band_images, pivots)
    found = picked
    for k in range(row_count.bit_length() - 2, 0, -1):
        found = found + exchange(found, "row", 1 << k)
    packed = pack(ordered, plans).reshape(part_count, narrow, line_dev * band_dev)
    arrived = lax.all_to_all(packed, AXES, 0, 0, tiled=True)
    for k in range(pix_count.bit_length() - 1):
        found = jnp.concatenate([found, exchange(found, "pix", 1 << k)], axis=0)
    found = found + exchange(found, "row", 1)
    keep, gains = factor(found, pix_count)
    return finish(arrived, keep, gains, plans, row_count, band_dev, line_dev)


def solution(mesh):
    placed = (P("pix", "row", None), P())
    return jax.shard_map(
        shards,
        mesh=mesh,
        in_specs=placed,
        out_specs=(P(AXES, None, None), P(None, AXES, None)),
        check_vma=False,
    )
```

time: 60 us -> 57.5 us (0.958)
  waiting for transfers between devices: 26.1 us -> 33.9 us
  Pallas kernels: 15.5 us -> 9.31 us
  starting transfers between devices: 16.7 us -> 13.2 us
  other arithmetic: 0.68 us -> 0.07 us
    ppermute x5, waiting for transfers between devices: 26.1 us -> 33.9 us  [exchange(): return lax.ppermute(x, axis, [(i, i ^ k) for i in range(count)])]
    pallas_call x1, Pallas kernels: 8.4 us -> 2.97 us  [factor(): pl.pallas_call(kernel, out_shape=(pltpu.VMEM((2 * bands, bands), bf16), p...]
    ppermute x5, starting transfers between devices: 9.37 us -> 5.89 us  [exchange(): return lax.ppermute(x, axis, [(i, i ^ k) for i in range(count)])]
    select_n x3 -> x0, other arithmetic: 0.67 us -> none  [shards(): jnp.where(after, jnp.concatenate([other, found], axis=0), jnp.concatenate...]
  transfers between devices with their start and end apart: 6 -> 6, of which waited for: 5 -> 5; matrix products, arithmetic and copies ran while one was open for 1% -> 0% of each run, Pallas kernels for 14% -> 5%
where the time goes in v1:
time: 57.5 us; the launch traced here: 57.2 us
  waiting for transfers between devices  33.9 us (59%)
  starting transfers between devices  13.2 us (23%)
  Pallas kernels  9.31 us (16%)
  between operations  0.69 us (1%)
    ppermute x5, waiting for transfers between devices, exchange(): return lax.ppermute(x, axis, [(i, i ^ k) for i in range(count)])  33.9 us
    all_to_all x1, starting transfers between devices, shards(): arrived = lax.all_to_all(packed, AXES, 0, 0, tiled=True)  7.33 us
    ppermute x5, starting transfers between devices, exchange(): return lax.ppermute(x, axis, [(i, i ^ k) for i in range(count)])  5.89 us
    pallas_call x1, Pallas kernels, factor(): pl.pallas_call(kernel, out_shape=(pltpu.VMEM((2 * bands, bands), bf16), p...  2.97 us
    pallas_call x1, Pallas kernels, finish(): pl.pallas_call(kernel, out_shape=(jax.ShapeDtypeStruct((narrow, lines, ba...  2.77 us
    pallas_call x1, Pallas kernels, pick(): pl.pallas_call(kernel, out_shape=(pltpu.VMEM((line_dev * band_dev, cols),...  2.28 us
    pallas_call x1, Pallas kernels, pack(): pl.pallas_call(kernel, out_shape=jax.ShapeDtypeStruct((cols, rows), bf16)...  1.29 us
  transfers between devices with their start and end apart: 6, of which 5 were waited for; matrix products, arithmetic and copies ran while one was open for 0% of the time, Pallas kernels for 5%

profile of v1, /device:TPU:0, one launch (start us, length us, event | category | flops | bytes accessed | tf_op | source)
XLA Modules:
  0.0 57.2 jit_solution(16556203646356843667)
XLA Ops:
  0.6 2.3 %pick.1 = (bf16[1024,512]{1,0:T(8,128)(2,1)S(1)}, bf16[32,64]{1,0:T(8,128)(2,1)S(1)}, bf16[768,256]{1,0:T(8,128)(2,1)S(1)}) custom-call(bf16[32,32,512]{2,1,0:T(8,128)(2,1)} %x_ref.1, s32[2,32]{1,0:T(2,128)} %far_ref.1), custom_call_target="tpu_custom_call" | custom-call | tf_op jit(solution)/shard_map/pick/pallas_call | solution.py:86
  2.9 1.3 %pack.1 = bf16[512,1024]{1,0:T(8,128)(2,1)} custom-call(bf16[1024,512]{1,0:T(8,128)(2,1)S(1)} %get-tuple-element.7.x_ref, bf16[768,256]{1,0:T(8,128)(2,1)S(1)} %get-tuple-element.8.plan_ref), custom_call_target="tpu_custom_call" | custom-call | tf_op jit(solution)/shard_map/pack/pallas_call | solution.py:127
  4.2 7.3 %all-to-all-start = ((bf16[32,16,1024]{2,1,0:T(8,128)(2,1)}), bf16[32,16,1024]{2,1,0:T(8,128)(2,1)S(1)}, u32[]{:S(2)}, u32[]{:S(2)}) async-start(bf16[32,16,1024]{2,1,0:T(8,128)(2,1)} %bitcast.1), calls=%async_computation | async-start | bytes 2097152 | tf_op jit(solution)/shard_map/all_to_all | solution.py:423
  11.6 2.7 %collective-permute-start = (bf16[32,64]{1,0:T(8,128)(2,1)S(1)}, bf16[32,64]{1,0:T(8,128)(2,1)S(1)}, u32[]{:S(2)}, u32[]{:S(2)}) collective-permute-start(bf16[32,64]{1,0:T(8,128)(2,1)S(1)} %get-tuple-element.9), channel_id=1, source_target_pairs={{0,2},{1,3},{2,0},{3,1},{4,6},{5,7},{6,4},{7,5},{8,10},{9,11},{10,... | collective-permute-start | bytes 12296 | tf_op jit(solution)/shard_map/ppermute | solution.py:339
  14.3 23.8 %collective-permute-done = bf16[32,64]{1,0:T(8,128)(2,1)S(1)} collective-permute-done((bf16[32,64]{1,0:T(8,128)(2,1)S(1)}, bf16[32,64]{1,0:T(8,128)(2,1)S(1)}, u32[]{:S(2)}, u32[]{:S(2)}) %collective-permute-start) | collective-permute-done | bytes 4128 | tf_op jit(solution)/shard_map/ppermute | solution.py:339
  38.1 0.0 collective-permute-start.1
  38.1 1.2 %collective-permute-done.1 = bf16[32,64]{1,0:T(8,128)(2,1)S(1)} collective-permute-done((bf16[32,64]{1,0:T(8,128)(2,1)S(1)}, bf16[32,64]{1,0:T(8,128)(2,1)S(1)}, u32[]{:S(2)}, u32[]{:S(2)}) %collective-permute-start.1) | collective-permute-done | bytes 4128 | tf_op jit(solution)/shard_map/ppermute | solution.py:339
  39.3 1.5 %collective-permute-start.2 = (bf16[64,64]{1,0:T(8,128)(2,1)S(1)}, bf16[64,64]{1,0:T(8,128)(2,1)S(1)}, u32[]{:S(2)}, u32[]{:S(2)}) collective-permute-start(bf16[64,64]{1,0:T(8,128)(2,1)S(1)} %pad_maximum_fusion.2), channel_id=1, source_target_pairs={{0,8},{4,12},{8,0},{12,4},{16,24},{20,28},{24,16},{28,20},{1,9},{5... | collective-permute-start | bytes 24584 | tf_op jit(solution)/shard_map/ppermute | solution.py:339
  40.8 2.3 %collective-permute-done.2 = bf16[64,64]{1,0:T(8,128)(2,1)S(1)} collective-permute-done((bf16[64,64]{1,0:T(8,128)(2,1)S(1)}, bf16[64,64]{1,0:T(8,128)(2,1)S(1)}, u32[]{:S(2)}, u32[]{:S(2)}) %collective-permute-start.2) | collective-permute-done | bytes 8224 | tf_op jit(solution)/shard_map/ppermute | solution.py:339
  43.1 1.5 %collective-permute-start.3 = (bf16[128,64]{1,0:T(8,128)(2,1)S(1)}, bf16[128,64]{1,0:T(8,128)(2,1)S(1)}, u32[]{:S(2)}, u32[]{:S(2)}) collective-permute-start(bf16[128,64]{1,0:T(8,128)(2,1)S(1)} %pad_maximum_fusion.1), channel_id=1, source_target_pairs={{0,16},{4,20},{8,24},{12,28},{16,0},{20,4},{24,8},{28,12},{1,17},{... | collective-permute-start | bytes 49160 | tf_op jit(solution)/shard_map/ppermute | solution.py:339
  44.7 2.4 %collective-permute-done.3 = bf16[128,64]{1,0:T(8,128)(2,1)S(1)} collective-permute-done((bf16[128,64]{1,0:T(8,128)(2,1)S(1)}, bf16[128,64]{1,0:T(8,128)(2,1)S(1)}, u32[]{:S(2)}, u32[]{:S(2)}) %collective-permute-start.3) | collective-permute-done | bytes 16416 | tf_op jit(solution)/shard_map/ppermute | solution.py:339
  47.1 0.1 collective-permute-start.4
  47.2 4.3 %collective-permute-done.4 = bf16[256,64]{1,0:T(8,128)(2,1)S(1)} collective-permute-done((bf16[256,64]{1,0:T(8,128)(2,1)S(1)}, bf16[256,64]{1,0:T(8,128)(2,1)S(1)}, u32[]{:S(2)}, u32[]{:S(2)}) %collective-permute-start.4) | collective-permute-done | bytes 32800 | tf_op jit(solution)/shard_map/ppermute | solution.py:339
  51.5 3.0 %factor.1 = (bf16[512,256]{1,0:T(8,128)(2,1)S(1)}, bf16[128,256]{1,0:T(8,128)(2,1)S(1)}) custom-call(bf16[256,64]{1,0:T(8,128)(2,1)S(1)} %fusion.s_ref), custom_call_target="tpu_custom_call" | custom-call | tf_op jit(solution)/shard_map/factor/pallas_call | solution.py:327
  54.5 0.0 all-to-all-done.a_ref
  54.5 2.8 %finish.1 = (bf16[16,128,256]{2,1,0:T(8,128)(2,1)}, bf16[64,16,128]{2,1,0:T(8,128)(2,1)}) custom-call(bf16[32,16,1024]{2,1,0:T(8,128)(2,1)S(1)} %all-to-all-done.a_ref, bf16[512,256]{1,0:T(8,128)(2,1)S(1)} %get-tuple-element.10.keep_ref, bf16[128,256]{1,0:T(8,128)(2,1)S(1)} %get-tuple-element.11.gain_ref, bf16[768,256]{1,0:T(8,128)(2,1)S(1)} %get-tuple-element.8.plan_ref), custom_call_target="tpu_custom_call" | custom-call | tf_op jit(solution)/shard_map/finish/pallas_call | solution.py:222
  (5 shorter events, 0.1 us)
Async XLA Ops:
  4.2 50.2 %all-to-all-start = ((bf16[32,16,1024]{2,1,0:T(8,128)(2,1)}), bf16[32,16,1024]{2,1,0:T(8,128)(2,1)S(1)}, u32[]{:S(2)}, u32[]{:S(2)}) async-start(bf16[32,16,1024]{2,1,0:T(8,128)(2,1)} %bitcast.1), calls=%async_computation | async-start | bytes 2097152 | tf_op jit(solution)/shard_map/all_to_all | solution.py:423
  11.6 26.6 %collective-permute-start = (bf16[32,64]{1,0:T(8,128)(2,1)S(1)}, bf16[32,64]{1,0:T(8,128)(2,1)S(1)}, u32[]{:S(2)}, u32[]{:S(2)}) collective-permute-start(bf16[32,64]{1,0:T(8,128)(2,1)S(1)} %get-tuple-element.9), channel_id=1, source_target_pairs={{0,2},{1,3},{2,0},{3,1},{4,6},{5,7},{6,4},{7,5},{8,10},{9,11},{10,... | collective-permute-start | bytes 12296 | tf_op jit(solution)/shard_map/ppermute | solution.py:339
  38.1 1.2 %collective-permute-start.1 = (bf16[32,64]{1,0:T(8,128)(2,1)S(1)}, bf16[32,64]{1,0:T(8,128)(2,1)S(1)}, u32[]{:S(2)}, u32[]{:S(2)}) collective-permute-start(bf16[32,64]{1,0:T(8,128)(2,1)S(1)} %add.6), channel_id=1, source_target_pairs={{0,4},{4,0},{8,12},{12,8},{16,20},{20,16},{24,28},{28,24},{1,5},{5... | collective-permute-start | bytes 12296 | tf_op jit(solution)/shard_map/ppermute | solution.py:339
  39.3 3.8 %collective-permute-start.2 = (bf16[64,64]{1,0:T(8,128)(2,1)S(1)}, bf16[64,64]{1,0:T(8,128)(2,1)S(1)}, u32[]{:S(2)}, u32[]{:S(2)}) collective-permute-start(bf16[64,64]{1,0:T(8,128)(2,1)S(1)} %pad_maximum_fusion.2), channel_id=1, source_target_pairs={{0,8},{4,12},{8,0},{12,4},{16,24},{20,28},{24,16},{28,20},{1,9},{5... | collective-permute-start | bytes 24584 | tf_op jit(solution)/shard_map/ppermute | solution.py:339
  43.1 4.0 %collective-permute-start.3 = (bf16[128,64]{1,0:T(8,128)(2,1)S(1)}, bf16[128,64]{1,0:T(8,128)(2,1)S(1)}, u32[]{:S(2)}, u32[]{:S(2)}) collective-permute-start(bf16[128,64]{1,0:T(8,128)(2,1)S(1)} %pad_maximum_fusion.1), channel_id=1, source_target_pairs={{0,16},{4,20},{8,24},{12,28},{16,0},{20,4},{24,8},{28,12},{1,17},{... | collective-permute-start | bytes 49160 | tf_op jit(solution)/shard_map/ppermute | solution.py:339
  47.1 4.3 %collective-permute-start.4 = (bf16[256,64]{1,0:T(8,128)(2,1)S(1)}, bf16[256,64]{1,0:T(8,128)(2,1)S(1)}, u32[]{:S(2)}, u32[]{:S(2)}) collective-permute-start(bf16[256,64]{1,0:T(8,128)(2,1)S(1)} %pad_maximum_fusion), channel_id=1, source_target_pairs={{0,1},{1,0},{2,3},{3,2},{4,5},{5,4},{6,7},{7,6},{8,9},{9,8},{10,11... | collective-permute-start | bytes 98312 | tf_op jit(solution)/shard_map/ppermute | solution.py:339

commit v2 on v1

--- a/solution.py
+++ b/solution.py
@@ -30,7 +30,7 @@
     return hot((size, size), lambda m, r: r == (m % outer) * inner + m // outer)
 
 
-def pick(band_images, pivots):
+def pack(band_images, pivots):
     band_dev, line_dev, cols = band_images.shape
     panels, panel = pivots.shape
     pivot_count = panels * panel
@@ -39,12 +39,18 @@
     shift = cols.bit_length() - 1
     chunks = band_dev // TILE
     rows = TILE * line_dev
+    every = band_dev * line_dev
     wide = TILE * TILE
-
-    def kernel(x_ref, far_ref, rows_ref, spec_ref, plan_ref, held_ref, piv_ref, sems):
+    sides = cols // wide
+
+    def kernel(x_ref, far_ref, out_ref, spec_ref, plan_ref, held_ref, piv_ref, rows_ref, out_buf, sems, out_sems):
         def copy(i):
             part = pl.ds(i * TILE, TILE)
             return pltpu.make_async_copy(x_ref.at[part], held_ref.at[part], sems.at[i])
+
+        def give(j, q):
+            part = (pl.ds(j * wide, wide), pl.ds(q * wide, wide))
+            return pltpu.make_async_copy(out_buf.at[part], out_ref.at[part], out_sems.at[j, q])
 
         indices = pltpu.make_async_copy(far_ref, piv_ref, sems.at[chunks])
         indices.start()
@@ -69,71 +75,62 @@
         lane = lax.broadcasted_iota(jnp.int32, (pivot_count, rows), 1)
         inside = lane % line_dev == inner
         fold = hot((TILE, rows), lambda b, r: r // line_dev == b)
-        for i in range(chunks):
-            copy(i).wait()
+
+        def find(i):
             bands = slice(i * TILE, (i + 1) * TILE)
             found = contract_last(chosen, held_ref[bands].reshape(rows, cols))
             found = jnp.where(inside, found, 0.0).astype(bf16)
             spec_ref[bands, :] = contract_last(fold, found).astype(bf16)
-            for h in range(line_dev // TILE):
-                block = held_ref[bands, h * TILE : (h + 1) * TILE, :].reshape(wide, cols)
-                block = jnp.dot(mixed, block, preferred_element_type=f32).astype(bf16)
-                for k in range(TILE):
-                    line = h * TILE + k
-                    start = ((line % groups) * taken + line // groups) * band_dev + i * TILE
-                    rows_ref[start : start + TILE, :] = block[k * TILE : (k + 1) * TILE]
+
+        for i in range(chunks):
+            copy(i).wait()
+            bands = slice(i * TILE, (i + 1) * TILE)
+            for side in range(0, cols, wide):
+                for h in range(line_dev // TILE):
+                    block = held_ref[bands, h * TILE : (h + 1) * TILE, side : side + wide].reshape(wide, wide)
+                    block = jnp.dot(mixed, block, preferred_element_type=f32).astype(bf16)
+                    for k in range(TILE):
+                        line = h * TILE + k
+                        start = ((line % groups) * taken + line // groups) * band_dev + i * TILE
+                        rows_ref[start : start + TILE, side : side + wide] = block[k * TILE : (k + 1) * TILE]
+            find(i)
+        for j in range(sides):
+            for q in range(every // wide):
+                side = slice(j * wide, (j + 1) * wide)
+                part = slice(q * wide, (q + 1) * wide)
+                out_buf[side, part] = contract_last(plan_ref[wide : 2 * wide], rows_ref[part, side]).astype(bf16)
+                give(j, q).start()
+        for j in range(sides):
+            for q in range(every // wide):
+                give(j, q).wait()
 
     return pl.pallas_call(
         kernel,
         out_shape=(
-            pltpu.VMEM((line_dev * band_dev, cols), bf16),
+            jax.ShapeDtypeStruct((cols, every), bf16),
             pltpu.VMEM((band_dev, pivot_count), bf16),
             pltpu.VMEM((3 * wide, wide), bf16),
         ),
         in_specs=[pl.BlockSpec(memory_space=pl.ANY), pl.BlockSpec(memory_space=pl.ANY)],
+        out_specs=(
+            pl.BlockSpec(memory_space=pl.ANY),
+            pl.BlockSpec(memory_space=pltpu.VMEM),
+            pl.BlockSpec(memory_space=pltpu.VMEM),
+        ),
         scratch_shapes=[
             pltpu.VMEM(band_images.shape, bf16),
             pltpu.VMEM(pivots.shape, pivots.dtype),
+            pltpu.VMEM((every, cols), bf16),
+            pltpu.VMEM((cols, every), bf16),
             pltpu.SemaphoreType.DMA((chunks + 1,)),
+            pltpu.SemaphoreType.DMA((sides, every // wide)),
         ],
-        name="pick",
+        name="pack",
     )(band_images, pivots)
 
 
 def near(*arrays):
     return [pltpu.with_memory_space_constraint(v, pltpu.VMEM) for v in arrays]
-
-
-def pack(ordered, plans):
-    rows, cols = ordered.shape
-    wide = plans.shape[1]
-    sides = cols // wide
-
-    def kernel(x_ref, plan_ref, out_ref, out_buf, sems):
-        def give(j, q):
-            part = (pl.ds(j * wide, wide), pl.ds(q * wide, wide))
-            return pltpu.make_async_copy(out_buf.at[part], out_ref.at[part], sems.at[j, q])
-
-        for j in range(sides):
-            for q in range(rows // wide):
-                side = slice(j * wide, (j + 1) * wide)
-                part = slice(q * wide, (q + 1) * wide)
-                out_buf[side, part] = contract_last(plan_ref[wide : 2 * wide], x_ref[part, side]).astype(bf16)
-                give(j, q).start()
-        for j in range(sides):
-            for q in range(rows // wide):
-                give(j, q).wait()
-
-    return pl.pallas_call(
-        kernel,
-        out_shape=jax.ShapeDtypeStruct((cols, rows), bf16),
-        out_specs=pl.BlockSpec(memory_space=pl.ANY),
-        scratch_shapes=[
-            pltpu.VMEM((cols, rows), bf16),
-            pltpu.SemaphoreType.DMA((sides, rows // wide)),
-        ],
-        name="pack",
-    )(*near(ordered, plans))
 
 
 def finish(arrived, keep, gains, plans, row_count, band_dev, line_dev):
@@ -146,6 +143,7 @@
     width = 4
     joined = bands // LANES
     pieces = narrow // width
+    halves = 2
 
     def swap(low, high, shift, mask):
         return (
@@ -161,38 +159,58 @@
         last = pltpu.make_async_copy(coef_buf, coef_ref, sems.at[pieces])
         lane = lax.broadcasted_iota(jnp.int32, (groups, LANES), 1)
         size = plan_ref.shape[1]
-        for r in range(row_count):
-            for j in range(joined):
-                sides = []
-                for n in range(taken // 2):
-                    tall = []
-                    for s in range(2):
-                        source = (j * taken + s * (taken // 2) + n) * row_count + r
-                        tall += [a_ref[source, :, g * LANES : (g + 1) * LANES] for g in range(groups)]
-                    sides.append(jnp.concatenate(tall, axis=0))
-                turned = jnp.dot(
-                    plan_ref[2 * size :], jnp.concatenate(sides, axis=1), preferred_element_type=f32
+
+        def project(p):
+            pixels = x_ref[p * width * lines : (p + 1) * width * lines, :]
+            both = jnp.dot(jnp.concatenate([pixels, pixels], axis=1), keep_ref[...], preferred_element_type=f32)
+            res_buf[p * width : (p + 1) * width] = both.astype(bf16).reshape(width, lines, bands)
+            give(p).start()
+
+        part = narrow // halves
+        short = part * groups
+
+        def gather(h, r, j):
+            top = 2 * size + h * short
+            mix = jnp.concatenate([plan_ref[top : top + short], plan_ref[top + size // 2 : top + size // 2 + short]], axis=0)
+            sides = []
+            for n in range(taken // 2):
+                tall = []
+                for s in range(2):
+                    source = (j * taken + s * (taken // 2) + n) * row_count + r
+                    tall += [a_ref[source, :, g * LANES : (g + 1) * LANES] for g in range(groups)]
+                sides.append(jnp.concatenate(tall, axis=0))
+            turned = jnp.dot(
+                mix, jnp.concatenate(sides, axis=1), preferred_element_type=f32
+            )
+            for c in range(part):
+                v = []
+                for i in range(taken):
+                    s, n = i // (taken // 2), i % (taken // 2)
+                    start = (s * part + c) * groups
+                    v.append(turned[start : start + groups, n * LANES : (n + 1) * LANES])
+                step = taken // 2
+                while step >= 1:
+                    shift = step * band_dev
+                    mask = (lane // shift) % 2 == 0
+                    w = list(v)
+                    for i in range(taken):
+                        if (i // step) % 2 == 0:
+                            w[i], w[i + step] = swap(v[i], v[i + step], shift, mask)
+                    v = w
+                    step //= 2
+                row = (h * part + c) * lines + r * line_dev
+                x_ref[row : row + line_dev, j * LANES : (j + 1) * LANES] = (
+                    jnp.concatenate(v, axis=0).astype(bf16)
                 )
-                for c in range(narrow):
-                    v = []
-                    for i in range(taken):
-                        s, n = i // (taken // 2), i % (taken // 2)
-                        start = (s * narrow + c) * groups
-                        v.append(turned[start : start + groups, n * LANES : (n + 1) * LANES])
-                    step = taken // 2
-                    while step >= 1:
-                        shift = step * band_dev
-                        mask = (lane // shift) % 2 == 0
-                        w = list(v)
-                        for i in range(taken):
-                            if (i // step) % 2 == 0:
-                                w[i], w[i + step] = swap(v[i], v[i + step], shift, mask)
-                        v = w
-                        step //= 2
-                    row = c * lines + r * line_dev
-                    x_ref[row : row + line_dev, j * LANES : (j + 1) * LANES] = (
-                        jnp.concatenate(v, axis=0).astype(bf16)
-                    )
+
+        places = [(r, j) for r in range(row_count) for j in range(joined)]
+        for h in range(halves):
+            for i, (r, j) in enumerate(places):
+                gather(h, r, j)
+                if False and (i + 1) * (pieces // halves) % len(places) == 0:
+                    project((h - 1) * (pieces // halves) + (i + 1) * (pieces // halves) // len(places) - 1)
+        for p in range(pieces // 2):
+            project(p)
         for c in range(0, narrow, 2):
             found = contract_last(gain_ref[...], x_ref[c * lines : (c + 2) * lines, :])
             found = (found[:kept] + found[kept:]).astype(bf16)
@@ -209,12 +227,8 @@
             coef_buf[k : k + narrow] = turned[:, :lines].reshape(narrow, narrow, lines)
             coef_buf[k + narrow : k + 2 * narrow] = turned[:, lines:].reshape(narrow, narrow, lines)
         last.start()
-        for p in range(pieces):
-            pixels = x_ref[p * width * lines : (p + 1) * width * lines, :]
-            both = jnp.dot(pixels, keep_ref[:bands], preferred_element_type=f32)
-            both = both + jnp.dot(pixels, keep_ref[bands:], preferred_element_type=f32)
-            res_buf[p * width : (p + 1) * width] = both.astype(bf16).reshape(width, lines, bands)
-            give(p).start()
+        for p in range(pieces // 2, pieces):
+            project(p)
         last.wait()
         for p in range(pieces):
             give(p).wait()
@@ -415,11 +429,10 @@
     )
     if not fits:
         return plain(band_images, line_index, column, pix_count, row_count, narrow)
-    ordered, picked, plans = pick(band_images, pivots)
-    found = picked
+    packed, found, plans = pack(band_images, pivots)
+    packed = packed.reshape(part_count, narrow, line_dev * band_dev)
     for k in range(row_count.bit_length() - 2, 0, -1):
         found = found + exchange(found, "row", 1 << k)
-    packed = pack(ordered, plans).reshape(part_count, narrow, line_dev * band_dev)
     arrived = lax.all_to_all(packed, AXES, 0, 0, tiled=True)
     for k in range(pix_count.bit_length() - 1):
         found = jnp.concatenate([found, exchange(found, "pix", 1 << k)], axis=0)

time: 57.5 us -> 57 us (level)
    pallas_call x2 -> x1, Pallas kernels: 3.57 us -> 3.29 us  [pack(): pl.pallas_call(kernel, out_shape=(jax.ShapeDtypeStruct((cols, every), bf1...]
where the time goes in v2:
time: 57 us; the launch traced here: 56.8 us
  waiting for transfers between devices  33.9 us (59%)
  starting transfers between devices  13.2 us (23%)
  Pallas kernels  8.88 us (16%)
  between operations  0.69 us (1%)
    ppermute x5, waiting for transfers between devices, exchange(): return lax.ppermute(x, axis, [(i, i ^ k) for i in range(count)])  33.9 us
    all_to_all x1, starting transfers between devices, shards(): arrived = lax.all_to_all(packed, AXES, 0, 0, tiled=True)  7.33 us
    ppermute x5, starting transfers between devices, exchange(): return lax.ppermute(x, axis, [(i, i ^ k) for i in range(count)])  5.89 us
    pallas_call x1, Pallas kernels, pack(): pl.pallas_call(kernel, out_shape=(jax.ShapeDtypeStruct((cols, every), bf1...  3.29 us
    pallas_call x1, Pallas kernels, factor(): pl.pallas_call(kernel, out_shape=(pltpu.VMEM((2 * bands, bands), bf16), p...  2.98 us
    pallas_call x1, Pallas kernels, finish(): pl.pallas_call(kernel, out_shape=(jax.ShapeDtypeStruct((narrow, lines, ba...  2.6 us
  transfers between devices with their start and end apart: 6, of which 5 were waited for; matrix products, arithmetic and copies ran while one was open for 0% of the time, Pallas kernels for 5%

profile of v2, /device:TPU:0, one launch (start us, length us, event | category | flops | bytes accessed | tf_op | source)
XLA Modules:
  0.0 56.8 jit_solution(10845389724444890300)
XLA Ops:
  0.6 3.3 %pack.1 = (bf16[512,1024]{1,0:T(8,128)(2,1)}, bf16[32,64]{1,0:T(8,128)(2,1)S(1)}, bf16[768,256]{1,0:T(8,128)(2,1)S(1)}) custom-call(bf16[32,32,512]{2,1,0:T(8,128)(2,1)} %x_ref.1, s32[2,32]{1,0:T(2,128)} %far_ref.1), custom_call_target="tpu_custom_call" | custom-call | tf_op jit(solution)/shard_map/pack/pallas_call | solution.py:107
  3.9 7.3 %all-to-all-start = ((bf16[32,16,1024]{2,1,0:T(8,128)(2,1)}), bf16[32,16,1024]{2,1,0:T(8,128)(2,1)S(1)}, u32[]{:S(2)}, u32[]{:S(2)}) async-start(bf16[32,16,1024]{2,1,0:T(8,128)(2,1)} %bitcast.1), calls=%async_computation | async-start | bytes 2097152 | tf_op jit(solution)/shard_map/all_to_all | solution.py:436
  11.3 2.7 %collective-permute-start = (bf16[32,64]{1,0:T(8,128)(2,1)S(1)}, bf16[32,64]{1,0:T(8,128)(2,1)S(1)}, u32[]{:S(2)}, u32[]{:S(2)}) collective-permute-start(bf16[32,64]{1,0:T(8,128)(2,1)S(1)} %get-tuple-element.8), channel_id=1, source_target_pairs={{0,2},{1,3},{2,0},{3,1},{4,6},{5,7},{6,4},{7,5},{8,10},{9,11},{10,... | collective-permute-start | bytes 12296 | tf_op jit(solution)/shard_map/ppermute | solution.py:353
  14.0 23.8 %collective-permute-done = bf16[32,64]{1,0:T(8,128)(2,1)S(1)} collective-permute-done((bf16[32,64]{1,0:T(8,128)(2,1)S(1)}, bf16[32,64]{1,0:T(8,128)(2,1)S(1)}, u32[]{:S(2)}, u32[]{:S(2)}) %collective-permute-start) | collective-permute-done | bytes 4128 | tf_op jit(solution)/shard_map/ppermute | solution.py:353
  37.8 0.0 collective-permute-start.1
  37.8 1.2 %collective-permute-done.1 = bf16[32,64]{1,0:T(8,128)(2,1)S(1)} collective-permute-done((bf16[32,64]{1,0:T(8,128)(2,1)S(1)}, bf16[32,64]{1,0:T(8,128)(2,1)S(1)}, u32[]{:S(2)}, u32[]{:S(2)}) %collective-permute-start.1) | collective-permute-done | bytes 4128 | tf_op jit(solution)/shard_map/ppermute | solution.py:353
  39.0 1.5 %collective-permute-start.2 = (bf16[64,64]{1,0:T(8,128)(2,1)S(1)}, bf16[64,64]{1,0:T(8,128)(2,1)S(1)}, u32[]{:S(2)}, u32[]{:S(2)}) collective-permute-start(bf16[64,64]{1,0:T(8,128)(2,1)S(1)} %pad_maximum_fusion.2), channel_id=1, source_target_pairs={{0,8},{4,12},{8,0},{12,4},{16,24},{20,28},{24,16},{28,20},{1,9},{5... | collective-permute-start | bytes 24584 | tf_op jit(solution)/shard_map/ppermute | solution.py:353
  40.5 2.3 %collective-permute-done.2 = bf16[64,64]{1,0:T(8,128)(2,1)S(1)} collective-permute-done((bf16[64,64]{1,0:T(8,128)(2,1)S(1)}, bf16[64,64]{1,0:T(8,128)(2,1)S(1)}, u32[]{:S(2)}, u32[]{:S(2)}) %collective-permute-start.2) | collective-permute-done | bytes 8224 | tf_op jit(solution)/shard_map/ppermute | solution.py:353
  42.8 1.5 %collective-permute-start.3 = (bf16[128,64]{1,0:T(8,128)(2,1)S(1)}, bf16[128,64]{1,0:T(8,128)(2,1)S(1)}, u32[]{:S(2)}, u32[]{:S(2)}) collective-permute-start(bf16[128,64]{1,0:T(8,128)(2,1)S(1)} %pad_maximum_fusion.1), channel_id=1, source_target_pairs={{0,16},{4,20},{8,24},{12,28},{16,0},{20,4},{24,8},{28,12},{1,17},{... | collective-permute-start | bytes 49160 | tf_op jit(solution)/shard_map/ppermute | solution.py:353
  44.4 2.4 %collective-permute-done.3 = bf16[128,64]{1,0:T(8,128)(2,1)S(1)} collective-permute-done((bf16[128,64]{1,0:T(8,128)(2,1)S(1)}, bf16[128,64]{1,0:T(8,128)(2,1)S(1)}, u32[]{:S(2)}, u32[]{:S(2)}) %collective-permute-start.3) | collective-permute-done | bytes 16416 | tf_op jit(solution)/shard_map/ppermute | solution.py:353
  46.8 0.1 collective-permute-start.4
  46.9 4.3 %collective-permute-done.4 = bf16[256,64]{1,0:T(8,128)(2,1)S(1)} collective-permute-done((bf16[256,64]{1,0:T(8,128)(2,1)S(1)}, bf16[256,64]{1,0:T(8,128)(2,1)S(1)}, u32[]{:S(2)}, u32[]{:S(2)}) %collective-permute-start.4) | collective-permute-done | bytes 32800 | tf_op jit(solution)/shard_map/ppermute | solution.py:353
  51.2 3.0 %factor.1 = (bf16[512,256]{1,0:T(8,128)(2,1)S(1)}, bf16[128,256]{1,0:T(8,128)(2,1)S(1)}) custom-call(bf16[256,64]{1,0:T(8,128)(2,1)S(1)} %fusion.s_ref), custom_call_target="tpu_custom_call" | custom-call | tf_op jit(solution)/shard_map/factor/pallas_call | solution.py:341
  54.2 0.0 all-to-all-done.a_ref
  54.2 2.6 %finish.1 = (bf16[16,128,256]{2,1,0:T(8,128)(2,1)}, bf16[64,16,128]{2,1,0:T(8,128)(2,1)}) custom-call(bf16[32,16,1024]{2,1,0:T(8,128)(2,1)S(1)} %all-to-all-done.a_ref, bf16[512,256]{1,0:T(8,128)(2,1)S(1)} %get-tuple-element.9.keep_ref, bf16[128,256]{1,0:T(8,128)(2,1)S(1)} %get-tuple-element.10.gain_ref, bf16[768,256]{1,0:T(8,128)(2,1)S(1)} %get-tuple-element.11.plan_ref), custom_call_target="tpu_custom_call" | custom-call | tf_op jit(solution)/shard_map/finish/pallas_call | solution.py:236
  (5 shorter events, 0.1 us)
Async XLA Ops:
  3.9 50.2 %all-to-all-start = ((bf16[32,16,1024]{2,1,0:T(8,128)(2,1)}), bf16[32,16,1024]{2,1,0:T(8,128)(2,1)S(1)}, u32[]{:S(2)}, u32[]{:S(2)}) async-start(bf16[32,16,1024]{2,1,0:T(8,128)(2,1)} %bitcast.1), calls=%async_computation | async-start | bytes 2097152 | tf_op jit(solution)/shard_map/all_to_all | solution.py:436
  11.3 26.6 %collective-permute-start = (bf16[32,64]{1,0:T(8,128)(2,1)S(1)}, bf16[32,64]{1,0:T(8,128)(2,1)S(1)}, u32[]{:S(2)}, u32[]{:S(2)}) collective-permute-start(bf16[32,64]{1,0:T(8,128)(2,1)S(1)} %get-tuple-element.8), channel_id=1, source_target_pairs={{0,2},{1,3},{2,0},{3,1},{4,6},{5,7},{6,4},{7,5},{8,10},{9,11},{10,... | collective-permute-start | bytes 12296 | tf_op jit(solution)/shard_map/ppermute | solution.py:353
  37.8 1.2 %collective-permute-start.1 = (bf16[32,64]{1,0:T(8,128)(2,1)S(1)}, bf16[32,64]{1,0:T(8,128)(2,1)S(1)}, u32[]{:S(2)}, u32[]{:S(2)}) collective-permute-start(bf16[32,64]{1,0:T(8,128)(2,1)S(1)} %add.6), channel_id=1, source_target_pairs={{0,4},{4,0},{8,12},{12,8},{16,20},{20,16},{24,28},{28,24},{1,5},{5... | collective-permute-start | bytes 12296 | tf_op jit(solution)/shard_map/ppermute | solution.py:353
  39.0 3.8 %collective-permute-start.2 = (bf16[64,64]{1,0:T(8,128)(2,1)S(1)}, bf16[64,64]{1,0:T(8,128)(2,1)S(1)}, u32[]{:S(2)}, u32[]{:S(2)}) collective-permute-start(bf16[64,64]{1,0:T(8,128)(2,1)S(1)} %pad_maximum_fusion.2), channel_id=1, source_target_pairs={{0,8},{4,12},{8,0},{12,4},{16,24},{20,28},{24,16},{28,20},{1,9},{5... | collective-permute-start | bytes 24584 | tf_op jit(solution)/shard_map/ppermute | solution.py:353
  42.8 4.0 %collective-permute-start.3 = (bf16[128,64]{1,0:T(8,128)(2,1)S(1)}, bf16[128,64]{1,0:T(8,128)(2,1)S(1)}, u32[]{:S(2)}, u32[]{:S(2)}) collective-permute-start(bf16[128,64]{1,0:T(8,128)(2,1)S(1)} %pad_maximum_fusion.1), channel_id=1, source_target_pairs={{0,16},{4,20},{8,24},{12,28},{16,0},{20,4},{24,8},{28,12},{1,17},{... | collective-permute-start | bytes 49160 | tf_op jit(solution)/shard_map/ppermute | solution.py:353
  46.8 4.3 %collective-permute-start.4 = (bf16[256,64]{1,0:T(8,128)(2,1)S(1)}, bf16[256,64]{1,0:T(8,128)(2,1)S(1)}, u32[]{:S(2)}, u32[]{:S(2)}) collective-permute-start(bf16[256,64]{1,0:T(8,128)(2,1)S(1)} %pad_maximum_fusion), channel_id=1, source_target_pairs={{0,1},{1,0},{2,3},{3,2},{4,5},{5,4},{6,7},{7,6},{8,9},{9,8},{10,11... | collective-permute-start | bytes 98312 | tf_op jit(solution)/shard_map/ppermute | solution.py:353
